TPU v7x, 32 devices: a whole 2x2x4 slice. The times are simulated.
32 devices in a mesh: dp: 8 (over y, x, core), tensor: 4 (over z).
Axes of the slice: x: 2, y: 2, z: 4, core: 2. Of those that a mesh axis runs over, the one named last changes fastest.
Arguments:
- grad_tokens: bfloat16 [1536, 2048], P('dp', 'tensor'), may hold values from -6 to 6
- hidden_input: bfloat16 [2048, 5120], P('dp', 'tensor'), may hold values from -6 to 6
- output_weight: bfloat16 [5120, 2048], P(None, 'tensor'), may hold values from -0.078125 to 0.078125
- image_tokens: int32 [8, 8], replicated, may hold values from 0 to 192, as said below
- moved_images: int32 [8], replicated, may hold values from 0 to 7, as said below
Outputs:
- input_grad: bfloat16 [2048, 5120], P('dp', 'tensor')
- weight_grad: float32 [5120, 2048], P('dp', 'tensor')
- bias_grad: float32 [2048], P('tensor')
Inputs may be any that keep to these rules, and one draw needn't show every extreme that they name: `image_tokens`: row s lists the merged tokens of sample s's images in order: 1 to 8 positive entries, then zeros; each row sums to 192. `moved_images`: entry s is less than the number of images of sample s; those trailing images hold at most 64 merged tokens together, exactly 64 for some sample in every draw. They are encoded by owner s + 1 (owner 0 after the last).
All inputs are finite; a program needn't handle non-finite values.
Results may differ from a plain program's by a relative error of at most 0.014.
Values may be sent and summed in bfloat16 or wider, within the bound.
A program may use at most 64 MiB of HBM per device.

v0:
```python
import jax
import jax.numpy as jnp
from jax import lax
from jax.sharding import PartitionSpec as P

root_half = 0.7071067811865476
inv_root_tau = 0.3989422804014327


def from_behind(value, axis, steps):
    count = lax.axis_size(axis)
    pairs = [(source, (source + steps) % count) for source in range(count)]
    return lax.ppermute(value, axis, pairs)


def gelu_parts(values):
    normal_cdf = 0.5 * (1.0 + jax.scipy.special.erf(values * root_half))
    density = jnp.exp(-0.5 * values * values) * inv_root_tau
    return (values * normal_cdf, normal_cdf + values * density)


def kept_lengths(image_tokens, moved_images):
    present = jnp.sum((image_tokens > 0).astype(jnp.int32), axis=1)
    slot_ids = jnp.arange(image_tokens.shape[1], dtype=jnp.int32)
    kept_mask = slot_ids[None, :] < (present - moved_images)[:, None]
    return jnp.sum(jnp.where(kept_mask, image_tokens, 0), axis=1)


def per_device(grad_tokens, hidden_input, output_weight, image_tokens, moved_images):
    dp_count = lax.axis_size("dp")
    dp_index = lax.axis_index("dp")
    tok_rows = grad_tokens.shape[0]
    buffer_rows = hidden_input.shape[0]
    tail_count = buffer_rows - tok_rows
    keep_len = kept_lengths(image_tokens, moved_images)
    own_keep = jnp.sum(jnp.where(jnp.arange(dp_count, dtype=jnp.int32) == dp_index, keep_len, 0))
    positions = jnp.arange(tok_rows, dtype=jnp.int32)[:, None]
    zero_value = jnp.zeros((), jnp.bfloat16)
    kept_rows = jnp.where(positions < own_keep, grad_tokens, zero_value)
    moving = jnp.where(
        positions[tok_rows - tail_count :] >= own_keep,
        grad_tokens[tok_rows - tail_count :],
        zero_value,
    )
    arrived = from_behind(moving, "dp", 1)
    grad_rows = jnp.concatenate([kept_rows, arrived], axis=0)
    bias_grad = lax.psum(jnp.sum(grad_tokens.astype(jnp.float32), axis=0), "dp")
    activation, slopes = gelu_parts(hidden_input.astype(jnp.float32))
    partials = lax.dot_general(
        grad_rows, output_weight, (((1,), (1,)), ((), ())), preferred_element_type=jnp.float32
    )
    grad_hidden = lax.psum_scatter(
        partials.astype(jnp.bfloat16), "tensor", scatter_dimension=1, tiled=True
    ).astype(jnp.float32)
    input_grad = (grad_hidden * slopes).astype(jnp.bfloat16)
    gathered_input = lax.all_gather(hidden_input, "tensor", axis=1, tiled=True)
    full_act = gelu_parts(gathered_input.astype(jnp.float32))[0].astype(jnp.bfloat16)
    hidden_width = full_act.shape[1]
    rows_each = (hidden_width + 8 * dp_count - 1) // (8 * dp_count) * 8
    padded = jnp.pad(full_act, ((0, 0), (0, rows_each * dp_count - hidden_width)))
    weight_grad = lax.psum_scatter(
        lax.dot_general(
            padded, grad_rows, (((0,), (0,)), ((), ())), preferred_element_type=jnp.float32
        ),
        "dp",
        scatter_dimension=0,
        tiled=True,
    )
    return (input_grad, weight_grad, bias_grad)


def solution(mesh):
    return jax.shard_map(
        per_device,
        mesh=mesh,
        in_specs=(P("dp", "tensor"), P("dp", "tensor"), P(None, "tensor"), P(), P()),
        out_specs=(P("dp", "tensor"), P("dp", "tensor"), P("tensor")),
        check_vma=False,
    )
```

profile of v0, /device:TPU:0, one launch (start us, length us, event | category | flops | bytes accessed | tf_op | source)
XLA Modules:
  0.0 212.5 jit_solution(6390169746239598268)
XLA Ops:
  7.2 0.0 all-gather.2.cloned.1.call-start
  7.2 0.7 all-gather.2.cloned.1.call-update
  7.9 0.0 reduce-scatter.3.cloned.1.call-start
  7.9 0.8 convert_reduce_fusion.1
  8.8 0.7 sub.3
  9.4 0.9 select_reduce_fusion
  10.3 0.6 fusion.17
  10.9 0.7 compare_bitcast_fusion
  11.6 0.9 slice_select_fusion
  12.5 0.5 collective-permute-start
  13.0 0.6 iota_compare_fusion.1
  13.7 1.0 broadcast_select_fusion
  14.7 3.1 %collective-permute-done = bf16[64,512]{1,0:T(8,128)(2,1)S(1)} collective-permute-done((bf16[64,512]{1,0:T(8,128)(2,1)S(1)}, bf16[64,512]{1,0:T(8,128)(2,1)S(1)}, u32[]{:S(2)}, u32[]{:S(2)}) %collective-permute-start) | collective-permute-done | bytes 65568 | tf_op jit(solution)/shard_map/ppermute | solution.py:13
  17.9 5.9 %convolution_convert_fusion = bf16[256,5120]{1,0:T(8,128)(2,1)} fusion(bf16[5120,512]{1,0:T(8,128)(2,1)} %param.7, bf16[64,512]{1,0:T(8,128)(2,1)S(1)} %collective-permute-done, bf16[192,512]{1,0:T(8,128)(2,1)S(1)} %broadcast_select_fusion), kind=kOutput, calls=%fused_computation.2 | convolution fusion | flops 1344012288 | bytes 8126464 | tf_op jit(solution)/shard_map/dot_general | solution.py:49
  23.8 0.0 reduce-scatter.3.cloned.1.call-update
  23.8 0.0 reduce-scatter.5.cloned.1.call-start
  23.8 43.2 %all-gather.2.cloned.1.call-done = bf16[256,5120]{1,0:T(8,128)(2,1)} async-done(((bf16[256,1280]{1,0:T(8,128)(2,1)}), bf16[256,5120]{1,0:T(8,128)(2,1)}) %all-gather.2.cloned.1.call-update) | async-done | bytes 2621456 | tf_op jit(solution)/shard_map/all_gather | solution.py:56
  67.0 7.3 %fusion.4 = f32[5120,512]{1,0:T(8,128)} fusion(bf16[256,5120]{1,0:T(8,128)(2,1)} %all-gather.2.cloned.1.call-done, bf16[64,512]{1,0:T(8,128)(2,1)S(1)} %collective-permute-done, bf16[192,512]{1,0:T(8,128)(2,1)S(1)} %broadcast_select_fusion), kind=kOutput, calls=%fused_computation.7 | convolution fusion | flops 1350565888 | bytes 13369344 | tf_op jit(solution)/shard_map/dot_general | solution.py:62
  74.4 0.0 copy-start.1
  74.4 0.0 copy-start
  74.4 0.0 reduce-scatter.5.cloned.1.call-update
  74.4 0.9 copy-done.1
  75.3 14.6 %psum.7 = f32[512]{0:T(512)} all-reduce(f32[512]{0:T(512)S(1)} %convert_reduce_fusion), channel_id=1, replica_groups=mesh['dp'=8,'tensor'=4] {'dp'}, use_global_device_ids=true, to_apply=%region_6.7 | all-reduce | flops 512 | bytes 4096 | tf_op jit(solution)/shard_map/psum | solution.py:47
  89.9 30.5 %reduce-scatter.3.cloned.1.call-done = bf16[256,1280]{1,0:T(8,128)(2,1)} async-done(((bf16[256,5120]{1,0:T(8,128)(2,1)}), bf16[256,1280]{1,0:T(8,128)(2,1)}) %reduce-scatter.3.cloned.1.call-update) | async-done | bytes 655376 | tf_op jit(solution)/shard_map/reduce_scatter | solution.py:52
  120.4 0.0 copy-done
  120.4 2.5 %fusion.16 = bf16[256,1280]{1,0:T(8,128)(2,1)} fusion(bf16[256,1280]{1,0:T(8,128)(2,1)S(1)} %copy-done, bf16[256,1280]{1,0:T(8,128)(2,1)} %reduce-scatter.3.cloned.1.call-done), kind=kLoop, calls=%fused_computation.22 | loop fusion | flops 3932160 | bytes 1966080 | tf_op jit(solution)/shard_map/convert_element_type | solution.py:55
  122.9 83.1 %reduce-scatter.5.cloned.1.call-done = f32[640,512]{1,0:T(8,128)} async-done(((f32[5120,512]{1,0:T(8,128)}), f32[640,512]{1,0:T(8,128)}) %reduce-scatter.5.cloned.1.call-update) | async-done | bytes 1310736 | tf_op jit(solution)/shard_map/reduce_scatter | solution.py:61
  (1 shorter events, 0.0 us)
Async XLA Ops:
  7.2 59.9 %all-gather.2.cloned.1.call-start = ((), (), s32[]{:S(2)}) async-start(), calls=%async_computation.3 | async-start | bytes 3276800 | tf_op jit(solution)/shard_map/all_gather | solution.py:56
  7.9 112.5 %reduce-scatter.3.cloned.1.call-start = ((), (), s32[]{:S(2)}) async-start(), calls=%async_computation.2 | async-start | bytes 3276800 | tf_op jit(solution)/shard_map/reduce_scatter | solution.py:52
  12.5 5.4 %collective-permute-start = (bf16[64,512]{1,0:T(8,128)(2,1)S(1)}, bf16[64,512]{1,0:T(8,128)(2,1)S(1)}, u32[]{:S(2)}, u32[]{:S(2)}) collective-permute-start(bf16[64,512]{1,0:T(8,128)(2,1)S(1)} %slice_select_fusion), channel_id=1, source_target_pairs={{0,4},{4,8},{8,12},{12,16},{16,20},{20,24},{24,28},{28,0},{1,5},{5... | collective-permute-start | bytes 196616 | tf_op jit(solution)/shard_map/ppermute | solution.py:13
  23.8 182.2 %reduce-scatter.5.cloned.1.call-start = ((), (), s32[]{:S(2)}) async-start(), calls=%async_computation.4 | async-start | bytes 11796480 | tf_op jit(solution)/shard_map/reduce_scatter | solution.py:61
  74.4 0.9 copy-start.1
  74.4 46.0 %copy-start = (bf16[256,1280]{1,0:T(8,128)(2,1)S(1)}, bf16[256,1280]{1,0:T(8,128)(2,1)}, u32[]{:S(2)}) copy-start(bf16[256,1280]{1,0:T(8,128)(2,1)} %param.6) | copy-start | bytes 1966084
Sparse Core Ops, SparseCore 0:
  9.5 57.4 all-gather.1
  69.3 51.0 reduce-scatter.2
  124.5 81.4 reduce-scatter.4
where the time goes:
time: 213 us
  waiting for transfers between devices  161 us (76%)
  blocking collectives  14.6 us (7%)
  between operations  13.8 us (6%)
  matrix products  13.2 us (6%)
  other arithmetic  8.8 us (4%)
    reduce_scatter x1, waiting for transfers between devices, per_device(): lax.psum_scatter(lax.dot_general(padded, grad_rows, (((0,), (0,)), ((), (...  83.1 us
    all_gather x1, waiting for transfers between devices, per_device(): gathered_input = lax.all_gather(hidden_input, 'tensor', axis=1, tiled=True)  43.2 us
    reduce_scatter x1, waiting for transfers between devices, per_device(): lax.psum_scatter(partials.astype(jnp.bfloat16), 'tensor', scatter_dimensi...  30.5 us
    psum x1, blocking collectives, per_device(): bias_grad = lax.psum(jnp.sum(grad_tokens.astype(jnp.float32), axis=0), 'dp')  14.6 us
    dot_general x1, matrix products, per_device(): lax.dot_general(padded, grad_rows, (((0,), (0,)), ((), ())), preferred_el...  7.31 us
    dot_general x1, matrix products, per_device(): lax.dot_general(grad_rows, output_weight, (((1,), (1,)), ((), ())), prefe...  5.9 us
  transfers between devices with their start and end apart: 4, of which 4 were waited for; matrix products, arithmetic and copies ran while one was open for 10% of the time, Pallas kernels for 0%

commit v1 on v0

--- a/solution.py
+++ b/solution.py
@@ -5,6 +5,17 @@
 
 root_half = 0.7071067811865476
 inv_root_tau = 0.3989422804014327
+
+
+def turned_line(x, name, d):
+    devices = lax.axis_size(name)
+    route = [(i, (i + 1) % devices) for i in range(devices)]
+    pieces = [x]
+    for reach in range(1, devices):
+        pieces = [lax.ppermute(pieces[0], name, route), *pieces]
+    out = jnp.concatenate(pieces, axis=d)
+    shift = (lax.axis_index(name) + 1) * pieces[-1].shape[d]
+    return jnp.roll(out, shift, axis=d)
 
 
 def from_behind(value, axis, steps):
@@ -53,7 +64,7 @@
         partials.astype(jnp.bfloat16), "tensor", scatter_dimension=1, tiled=True
     ).astype(jnp.float32)
     input_grad = (grad_hidden * slopes).astype(jnp.bfloat16)
-    gathered_input = lax.all_gather(hidden_input, "tensor", axis=1, tiled=True)
+    gathered_input = turned_line(hidden_input, "tensor", 1)
     full_act = gelu_parts(gathered_input.astype(jnp.float32))[0].astype(jnp.bfloat16)
     hidden_width = full_act.shape[1]
     rows_each = (hidden_width + 8 * dp_count - 1) // (8 * dp_count) * 8

time: 213 us -> 206 us (0.967)
  waiting for transfers between devices: 161 us -> 138 us
  starting transfers between devices: 0.66 us -> 19.2 us
  blocking collectives: 14.6 us -> 12.4 us
    ppermute x0 -> x3, waiting for transfers between devices: none -> 69.9 us  [turned_line(): pieces = [lax.ppermute(pieces[0], name, route), *pieces]]
    all_gather x1 -> x0, waiting for transfers between devices: 43.2 us -> none  [per_device(): gathered_input = lax.all_gather(hidden_input, 'tensor', axis=1, tiled=True)]
    reduce_scatter x1, waiting for transfers between devices: 30.5 us -> 0.01 us  [per_device(): lax.psum_scatter(partials.astype(jnp.bfloat16), 'tensor', scatter_dimensi...]
    ppermute x0 -> x3, starting transfers between devices: none -> 18.6 us  [turned_line(): pieces = [lax.ppermute(pieces[0], name, route), *pieces]]
    reduce_scatter x1, waiting for transfers between devices: 83.1 us -> 64.7 us  [per_device(): lax.psum_scatter(lax.dot_general(padded, grad_rows, (((0,), (0,)), ((), (...]
    psum x1, blocking collectives: 14.6 us -> 12.4 us  [per_device(): bias_grad = lax.psum(jnp.sum(grad_tokens.astype(jnp.float32), axis=0), 'dp')]
  transfers between devices with their start and end apart: 4 -> 6, of which waited for: 4 -> 5; matrix products, arithmetic and copies ran while one was open for 10% -> 5% of each run, Pallas kernels for 0% -> 0%
where the time goes in v1:
time: 206 us; the launch traced here: 205 us
  waiting for transfers between devices  138 us (67%)
  starting transfers between devices  19.2 us (9%)
  between operations  14.2 us (7%)
  blocking collectives  12.4 us (6%)
  matrix products  11.6 us (6%)
  other arithmetic  8.88 us (4%)
    ppermute x3, waiting for transfers between devices, turned_line(): pieces = [lax.ppermute(pieces[0], name, route), *pieces]  69.9 us
    reduce_scatter x1, waiting for transfers between devices, per_device(): lax.psum_scatter(lax.dot_general(padded, grad_rows, (((0,), (0,)), ((), (...  64.7 us
    ppermute x3, starting transfers between devices, turned_line(): pieces = [lax.ppermute(pieces[0], name, route), *pieces]  18.6 us
    psum x1, blocking collectives, per_device(): bias_grad = lax.psum(jnp.sum(grad_tokens.astype(jnp.float32), axis=0), 'dp')  12.4 us
    dot_general x1, matrix products, per_device(): lax.dot_general(padded, grad_rows, (((0,), (0,)), ((), ())), preferred_el...  6.07 us
    dot_general x1, matrix products, per_device(): lax.dot_general(grad_rows, output_weight, (((1,), (1,)), ((), ())), prefe...  5.56 us
  transfers between devices with their start and end apart: 6, of which 5 were waited for; matrix products, arithmetic and copies ran while one was open for 5% of the time, Pallas kernels for 0%

profile of v1, /device:TPU:0, one launch (start us, length us, event | category | flops | bytes accessed | tf_op | source)
XLA Modules:
  0.0 205.5 jit_solution(14021581415114108127)
XLA Ops:
  7.2 0.0 reduce-scatter.3.cloned.1.call-start
  7.2 0.8 convert_reduce_fusion.1
  8.0 0.7 sub.7
  8.7 0.9 select_reduce_fusion
  9.5 0.6 fusion.18
  10.2 0.7 compare_bitcast_fusion
  10.8 0.9 slice_select_fusion
  11.8 0.5 collective-permute-start
  12.3 0.6 iota_compare_fusion.1
  13.0 1.0 broadcast_select_fusion
  14.0 0.0 copy-start
  14.0 3.1 %collective-permute-done = bf16[64,512]{1,0:T(8,128)(2,1)S(1)} collective-permute-done((bf16[64,512]{1,0:T(8,128)(2,1)S(1)}, bf16[64,512]{1,0:T(8,128)(2,1)S(1)}, u32[]{:S(2)}, u32[]{:S(2)}) %collective-permute-start) | collective-permute-done | bytes 65568 | tf_op jit(solution)/shard_map/ppermute | solution.py:24
  17.1 5.6 %convolution_convert_fusion = bf16[256,5120]{1,0:T(8,128)(2,1)} fusion(bf16[5120,512]{1,0:T(8,128)(2,1)} %param.7, bf16[64,512]{1,0:T(8,128)(2,1)S(1)} %collective-permute-done, bf16[192,512]{1,0:T(8,128)(2,1)S(1)} %broadcast_select_fusion), kind=kOutput, calls=%fused_computation.2 | convolution fusion | flops 1344012288 | bytes 8126464 | tf_op jit(solution)/shard_map/dot_general | solution.py:60
  22.7 0.0 reduce-scatter.3.cloned.1.call-update
  22.7 0.0 reduce-scatter.5.cloned.1.call-start
  22.8 0.0 copy-done
  22.8 2.4 %collective-permute-start.1 = (bf16[256,1280]{1,0:T(8,128)(2,1)S(1)}, bf16[256,1280]{1,0:T(8,128)(2,1)S(1)}, u32[]{:S(2)}, u32[]{:S(2)}) collective-permute-start(bf16[256,1280]{1,0:T(8,128)(2,1)S(1)} %copy-done), channel_id=1, source_target_pairs={{0,1},{1,2},{2,3},{3,0},{4,5},{5,6},{6,7},{7,4},{8,9},{9,10},{10,1... | collective-permute-start | bytes 1966088 | tf_op jit(solution)/shard_map/ppermute | solution.py:15
  25.2 24.7 %collective-permute-done.1 = bf16[256,1280]{1,0:T(8,128)(2,1)S(1)} collective-permute-done((bf16[256,1280]{1,0:T(8,128)(2,1)S(1)}, bf16[256,1280]{1,0:T(8,128)(2,1)S(1)}, u32[]{:S(2)}, u32[]{:S(2)}) %collective-permute-start.1) | collective-permute-done | bytes 655392 | tf_op jit(solution)/shard_map/ppermute | solution.py:15
  49.9 8.8 %collective-permute-start.2 = (bf16[256,1280]{1,0:T(8,128)(2,1)S(1)}, bf16[256,1280]{1,0:T(8,128)(2,1)S(1)}, u32[]{:S(2)}, u32[]{:S(2)}) collective-permute-start(bf16[256,1280]{1,0:T(8,128)(2,1)S(1)} %collective-permute-done.1), channel_id=1, source_target_pairs={{0,1},{1,2},{2,3},{3,0},{4,5},{5,6},{6,7},{7,4},{8,9},{9,10},{10,1... | collective-permute-start | bytes 1966088 | tf_op jit(solution)/shard_map/ppermute | solution.py:15
  58.7 29.4 %collective-permute-done.2 = bf16[256,1280]{1,0:T(8,128)(2,1)S(1)} collective-permute-done((bf16[256,1280]{1,0:T(8,128)(2,1)S(1)}, bf16[256,1280]{1,0:T(8,128)(2,1)S(1)}, u32[]{:S(2)}, u32[]{:S(2)}) %collective-permute-start.2) | collective-permute-done | bytes 655392 | tf_op jit(solution)/shard_map/ppermute | solution.py:15
  88.1 7.4 %collective-permute-start.3 = (bf16[256,1280]{1,0:T(8,128)(2,1)S(1)}, bf16[256,1280]{1,0:T(8,128)(2,1)S(1)}, u32[]{:S(2)}, u32[]{:S(2)}) collective-permute-start(bf16[256,1280]{1,0:T(8,128)(2,1)S(1)} %collective-permute-done.2), channel_id=1, source_target_pairs={{0,1},{1,2},{2,3},{3,0},{4,5},{5,6},{6,7},{7,4},{8,9},{9,10},{10,1... | collective-permute-start | bytes 1966088 | tf_op jit(solution)/shard_map/ppermute | solution.py:15
  95.4 15.8 %collective-permute-done.3 = bf16[256,1280]{1,0:T(8,128)(2,1)S(1)} collective-permute-done((bf16[256,1280]{1,0:T(8,128)(2,1)S(1)}, bf16[256,1280]{1,0:T(8,128)(2,1)S(1)}, u32[]{:S(2)}, u32[]{:S(2)}) %collective-permute-start.3) | collective-permute-done | bytes 655392 | tf_op jit(solution)/shard_map/ppermute | solution.py:15
  111.2 0.1 constant_dynamic-update-slice_fusion.7
  111.3 0.1 constant_dynamic-update-slice_fusion.6
  111.4 0.1 constant_dynamic-update-slice_fusion.5
  111.5 0.1 constant_dynamic-update-slice_fusion.4
  111.5 0.1 constant_dynamic-update-slice_fusion.3
  111.6 0.1 constant_dynamic-update-slice_fusion.2
  111.7 0.1 constant_dynamic-update-slice_fusion.1
  111.8 0.1 constant_dynamic-update-slice_fusion
  111.9 6.1 %fusion.4 = f32[5120,512]{1,0:T(8,128)} fusion(bf16[256,10240]{1,0:T(8,128)(2,1)S(1)} %constant_dynamic-update-slice_fusion, s32[]{:T(128)S(6)} %select_n.34, bf16[64,512]{1,0:T(8,128)(2,1)S(1)} %collective-permute-done, bf16[192,512]{1,0:T(8,128)(2,1)S(1)} %broadcast_select_fusion), kind=kOutput, calls=%fused_computation.7 | convolution fusion | flops 1350565888 | bytes 13369348 | tf_op jit(solution)/shard_map/dot_general | solution.py:73
  117.9 0.0 copy-start.1
  117.9 0.0 reduce-scatter.5.cloned.1.call-update
  118.0 0.9 copy-done.1
  118.9 12.4 %psum.7 = f32[512]{0:T(512)} all-reduce(f32[512]{0:T(512)S(1)} %convert_reduce_fusion), channel_id=1, replica_groups=mesh['dp'=8,'tensor'=4] {'dp'}, use_global_device_ids=true, to_apply=%region_6.7 | all-reduce | flops 512 | bytes 4096 | tf_op jit(solution)/shard_map/psum | solution.py:58
  131.3 0.0 reduce-scatter.3.cloned.1.call-done
  131.3 2.6 %fusion.17 = bf16[256,1280]{1,0:T(8,128)(2,1)} fusion(bf16[256,1280]{1,0:T(8,128)(2,1)S(1)} %copy-done, bf16[256,1280]{1,0:T(8,128)(2,1)} %reduce-scatter.3.cloned.1.call-done), kind=kLoop, calls=%fused_computation.23 | loop fusion | flops 3932160 | bytes 1966080 | tf_op jit(solution)/shard_map/convert_element_type | solution.py:66
  133.9 64.7 %reduce-scatter.5.cloned.1.call-done = f32[640,512]{1,0:T(8,128)} async-done(((f32[5120,512]{1,0:T(8,128)}), f32[640,512]{1,0:T(8,128)}) %reduce-scatter.5.cloned.1.call-update) | async-done | bytes 1310736 | tf_op jit(solution)/shard_map/reduce_scatter | solution.py:72
  (1 shorter events, 0.0 us)
Async XLA Ops:
  7.2 124.1 %reduce-scatter.3.cloned.1.call-start = ((), (), s32[]{:S(2)}) async-start(), calls=%async_computation.2 | async-start | bytes 3276800 | tf_op jit(solution)/shard_map/reduce_scatter | solution.py:63
  11.8 5.4 %collective-permute-start = (bf16[64,512]{1,0:T(8,128)(2,1)S(1)}, bf16[64,512]{1,0:T(8,128)(2,1)S(1)}, u32[]{:S(2)}, u32[]{:S(2)}) collective-permute-start(bf16[64,512]{1,0:T(8,128)(2,1)S(1)} %slice_select_fusion), channel_id=1, source_target_pairs={{0,4},{4,8},{8,12},{12,16},{16,20},{20,24},{24,28},{28,0},{1,5},{5... | collective-permute-start | bytes 196616 | tf_op jit(solution)/shard_map/ppermute | solution.py:24
  14.0 8.8 %copy-start = (bf16[256,1280]{1,0:T(8,128)(2,1)S(1)}, bf16[256,1280]{1,0:T(8,128)(2,1)}, u32[]{:S(2)}) copy-start(bf16[256,1280]{1,0:T(8,128)(2,1)} %param.6) | copy-start | bytes 1966084
  22.7 175.9 %reduce-scatter.5.cloned.1.call-start = ((), (), s32[]{:S(2)}) async-start(), calls=%async_computation.3 | async-start | bytes 11796480 | tf_op jit(solution)/shard_map/reduce_scatter | solution.py:72
  22.8 27.1 %collective-permute-start.1 = (bf16[256,1280]{1,0:T(8,128)(2,1)S(1)}, bf16[256,1280]{1,0:T(8,128)(2,1)S(1)}, u32[]{:S(2)}, u32[]{:S(2)}) collective-permute-start(bf16[256,1280]{1,0:T(8,128)(2,1)S(1)} %copy-done), channel_id=1, source_target_pairs={{0,1},{1,2},{2,3},{3,0},{4,5},{5,6},{6,7},{7,4},{8,9},{9,10},{10,1... | collective-permute-start | bytes 1966088 | tf_op jit(solution)/shard_map/ppermute | solution.py:15
  49.9 38.2 %collective-permute-start.2 = (bf16[256,1280]{1,0:T(8,128)(2,1)S(1)}, bf16[256,1280]{1,0:T(8,128)(2,1)S(1)}, u32[]{:S(2)}, u32[]{:S(2)}) collective-permute-start(bf16[256,1280]{1,0:T(8,128)(2,1)S(1)} %collective-permute-done.1), channel_id=1, source_target_pairs={{0,1},{1,2},{2,3},{3,0},{4,5},{5,6},{6,7},{7,4},{8,9},{9,10},{10,1... | collective-permute-start | bytes 1966088 | tf_op jit(solution)/shard_map/ppermute | solution.py:15
  88.1 23.2 %collective-permute-start.3 = (bf16[256,1280]{1,0:T(8,128)(2,1)S(1)}, bf16[256,1280]{1,0:T(8,128)(2,1)S(1)}, u32[]{:S(2)}, u32[]{:S(2)}) collective-permute-start(bf16[256,1280]{1,0:T(8,128)(2,1)S(1)} %collective-permute-done.2), channel_id=1, source_target_pairs={{0,1},{1,2},{2,3},{3,0},{4,5},{5,6},{6,7},{7,4},{8,9},{9,10},{10,1... | collective-permute-start | bytes 1966088 | tf_op jit(solution)/shard_map/ppermute | solution.py:15
  117.9 0.9 copy-start.1
Sparse Core Ops, SparseCore 0:
  22.8 77.0 reduce-scatter.2
  118.1 80.5 reduce-scatter.4
